TPU v7x, 256 devices: a whole 4x4x8 slice. The times are simulated.
256 devices in a mesh: dp: 16 (over x, z_lo), hyper: 16 (over y, z_hi, core).
Axes of the slice: x: 4, y: 4, z: 8 (z_hi: 2, z_lo: 4; z = z_hi * 4 + z_lo), core: 2. Of those that a mesh axis runs over, the one named last changes fastest.
Arguments:
- inputs: bfloat16 [512, 64, 128], P(('dp', 'hyper')), may hold values from -64 to 64
- labels: int32 [512, 64], P(('dp', 'hyper')), may hold values from 0 to 255
- client_ids: int32 [512], P(('dp', 'hyper')), may hold values from 0 to 511
- ext_weight: bfloat16 [128, 4096], replicated, may hold values from -0.5 to 0.5
- ext_bias: bfloat16 [4096], replicated, may hold values from -3 to 3
- embeddings: bfloat16 [512, 128], replicated, may hold values from -1.5 to 1.5
- hyper_in: bfloat16 [128, 50], replicated, may hold values from -2.09375 to 2.09375
- hyper_bias: float32 [50], replicated, may hold values from -3 to 3
- hyper_out: bfloat16 [4096, 50, 256], P('hyper'), may hold values from -0.1796875 to 0.1796875
Outputs:
- grad_ext_weight: float32 [128, 4096], replicated
- grad_ext_bias: float32 [4096], replicated
- grad_embeddings: float32 [512, 128], replicated
- grad_hyper_in: float32 [128, 50], replicated
- grad_hyper_bias: float32 [50], replicated
- grad_hyper_out: float32 [4096, 50, 256], P(('hyper', 'dp'))
Inputs may be any that keep to these rules, and one draw needn't show every extreme that they name: `client_ids`: A client may hold several slots or none.
All inputs are finite; a program needn't handle non-finite values.
Results may differ from a plain program's by a relative error of at most 0.014.
The roundings to bfloat16 on the way count: a program that leaves them out, or rounds other values in their place, can miss the bound.
Values may be sent and summed in bfloat16 or wider, within the bound.
No kernel may reach another device: no remote copies, remote signals or barrier semaphores. Data moves between devices by JAX's collectives and lax.ppermute only.
A program may use at most 128 MiB of HBM per device.

v0:
```python
import jax
import jax.numpy as jnp
from jax import lax
from jax.sharding import Mesh
from jax.sharding import PartitionSpec as P

DP = ("dp_0", "dp_1")
DP_HYPER = ("dp_0", "dp_1", "hyper")
HYPER_DP = ("hyper", "dp_0", "dp_1")


def sent_to_all(value, axis):
    copies = jnp.broadcast_to(value, (lax.axis_size(axis), *value.shape))
    return lax.all_to_all(copies, axis, split_axis=0, concat_axis=0, tiled=True)


def laid_out(tiles, dim):
    lengths = list(tiles.shape[1:])
    lengths[dim] *= tiles.shape[0]
    return jnp.moveaxis(tiles, 0, dim).reshape(lengths)


def gather_directly(value, axis, dim):
    tiles = sent_to_all(value, axis)
    return laid_out(tiles, dim)


def own_rows(terms, axes):
    total = terms.astype(jnp.bfloat16)
    for axis in axes:
        total = lax.psum_scatter(total, axis, scatter_dimension=0, tiled=True)
    return total.astype(jnp.float32)


def silu_slope(values):
    logistic = jax.nn.sigmoid(values)
    return logistic * (1.0 + values * (1.0 - logistic))


def class_grads(logits, slot_labels, row_count):
    largest = jnp.max(logits, axis=-1, keepdims=True)
    exponent = jnp.exp(logits - largest)
    probability = exponent / jnp.sum(exponent, axis=-1, keepdims=True)
    classes = jnp.arange(logits.shape[-1], dtype=jnp.int32)
    onehot = (slot_labels[..., None] == classes).astype(jnp.float32)
    return ((probability - onehot) / row_count).astype(jnp.bfloat16)


def local(
    inputs, labels, client_ids, ext_weight, ext_bias, embeddings, hyper_in, hyper_bias, hyper_out
):
    slot_count, row_count, width_in = inputs.shape
    width = ext_weight.shape[1]
    flat_in = inputs.reshape(slot_count * row_count, width_in)
    preact = jnp.dot(flat_in, ext_weight, preferred_element_type=jnp.float32) + ext_bias.astype(
        jnp.float32
    )
    features = jax.nn.silu(preact).astype(jnp.bfloat16).reshape(slot_count, row_count, width)
    row_ids = gather_directly(client_ids, "hyper", 0)
    table_ids = jnp.arange(embeddings.shape[0], dtype=jnp.int32)
    select = (row_ids[:, None] == table_ids[None, :]).astype(jnp.bfloat16)
    picked = jnp.dot(select, embeddings, preferred_element_type=jnp.float32).astype(jnp.bfloat16)
    hyper_preact = jnp.dot(picked, hyper_in, preferred_element_type=jnp.float32) + hyper_bias
    hidden = jax.nn.silu(hyper_preact).astype(jnp.bfloat16)
    head_part = jnp.einsum(
        "kh,dhc->kdc", hidden, hyper_out, preferred_element_type=jnp.float32
    ).astype(jnp.bfloat16)
    feat_cols = lax.all_to_all(features, "hyper", split_axis=2, concat_axis=0, tiled=True)
    logits = lax.psum_scatter(
        jnp.einsum("krd,kdc->krc", feat_cols, head_part, preferred_element_type=jnp.float32),
        "hyper",
        scatter_dimension=0,
        tiled=True,
    )
    dlogits = class_grads(logits, labels, row_count)
    dlog_rows = lax.all_gather(dlogits, "hyper", axis=0, tiled=True)
    dhead_part = jnp.einsum(
        "krd,krc->kdc", feat_cols, dlog_rows, preferred_element_type=jnp.float32
    ).astype(jnp.bfloat16)
    dfeat_cols = jnp.einsum(
        "krc,kdc->krd", dlog_rows, head_part, preferred_element_type=jnp.float32
    ).astype(jnp.bfloat16)
    dfeatures = lax.all_to_all(dfeat_cols, "hyper", split_axis=0, concat_axis=2, tiled=True)
    dpreact = (
        dfeatures.reshape(slot_count * row_count, width).astype(jnp.float32) * silu_slope(preact)
    ).astype(jnp.bfloat16)
    grad_weight = jnp.dot(flat_in.T, dpreact, preferred_element_type=jnp.float32)
    grad_bias = jnp.sum(dpreact.astype(jnp.float32), axis=0)
    grad_out = own_rows(
        jnp.einsum("kh,kdc->dhc", hidden, dhead_part, preferred_element_type=jnp.float32), DP
    )
    dhidden = jnp.einsum("kdc,dhc->kh", dhead_part, hyper_out, preferred_element_type=jnp.float32)
    hyper_dpre = dhidden * silu_slope(hyper_preact)
    grad_in = jnp.dot(picked.astype(jnp.float32).T, hyper_dpre)
    grad_hbias = jnp.sum(hyper_dpre, axis=0)
    back_rows = jnp.dot(hyper_dpre, hyper_in.astype(jnp.float32).T)
    grad_table = jnp.dot(select.astype(jnp.float32).T, back_rows)
    grad_weight, grad_bias, grad_table, grad_in, grad_hbias = lax.psum(
        (grad_weight, grad_bias, grad_table, grad_in, grad_hbias), DP_HYPER
    )
    return (grad_weight, grad_bias, grad_table, grad_in, grad_hbias, grad_out)


def solution(mesh):
    torus = Mesh(mesh.devices.reshape(4, 4, mesh.shape["hyper"]), ("dp_0", "dp_1", "hyper"))
    placed = (
        P(DP_HYPER, None, None),
        P(DP_HYPER, None),
        P(DP_HYPER),
        P(),
        P(),
        P(),
        P(),
        P(),
        P("hyper", None, None),
    )
    return jax.shard_map(
        local,
        mesh=torus,
        in_specs=placed,
        out_specs=(P(), P(), P(), P(), P(), P(HYPER_DP, None, None)),
        check_vma=False,
    )
```

profile of v0, /device:TPU:1, one launch (start us, length us, event | category | flops | bytes accessed | tf_op | source)
XLA Modules:
  0.0 629.8 jit_solution(14461696702569586145)
XLA Ops:
  7.2 1.3 broadcast_in_dim.2
  8.5 12.6 %all-to-all-start.1 = ((s32[16,1,2]{2,1,0:T(1,128)}), s32[16,1,2]{2,1,0:T(1,128)S(1)}, u32[]{:S(2)}, u32[]{:S(2)}) async-start(s32[16,1,2]{2,1,0:T(1,128)} %broadcast_in_dim.2), calls=%async_computation.1 | async-start | bytes 16384 | tf_op jit(solution)/shard_map/all_to_all | solution.py:14
  21.1 0.7 convert_element_type.58
  21.8 3.1 multiply_convert_fusion.1
  24.9 5.0 copy.35
  30.0 2.2 reshape.50
  32.3 9.6 %all-to-all-start = ((bf16[16,2,16384]{2,1,0:T(2,128)(2,1)}), bf16[16,2,16384]{2,1,0:T(2,128)(2,1)S(1)}, u32[]{:S(2)}, u32[]{:S(2)}) async-start(bf16[16,2,16384]{2,1,0:T(2,128)(2,1)} %reshape.50), calls=%async_computation | async-start | bytes 2097152 | tf_op jit(solution)/shard_map/all_to_all | solution.py:68
  41.9 0.0 reduce-scatter.4.cloned.1.call-start
  41.9 0.5 broadcast.18
  42.4 0.7 reduce.3
  43.1 0.1 eq.28
  43.2 0.2 convolution_convert_fusion.1
  43.4 0.1 convolution_add_fusion.1
  43.6 10.5 %fusion.9 = bf16[32,256,256]{2,0,1:T(8,128)(2,1)} fusion(bf16[256,50,256]{2,0,1:T(8,128)(2,1)} %param.17, f32[32,50]{1,0:T(8,128)S(1)} %convolution_add_fusion.1), kind=kOutput, calls=%fused_computation.12 | convolution fusion | flops 211820352 | bytes 10754304 | tf_op jit(solution)/shard_map/kh,dhc->kdc/dot_general | solution.py:65
  54.1 9.6 %all-to-all-done = bf16[16,2,16384]{2,1,0:T(2,128)(2,1)S(1)} async-done(((bf16[16,2,16384]{2,1,0:T(2,128)(2,1)}), bf16[16,2,16384]{2,1,0:T(2,128)(2,1)S(1)}, u32[]{:S(2)}, u32[]{:S(2)}) %all-to-all-start) | async-done | bytes 1048608 | tf_op jit(solution)/shard_map/all_to_all | solution.py:68
  63.7 2.4 reshape.51
  66.1 4.5 copy.36
  70.6 6.0 fusion.7
  76.5 0.0 reduce-scatter.4.cloned.1.call-update
  76.6 0.0 all-gather.2.cloned.1.call-start
  76.6 89.9 %reduce-scatter.4.cloned.1.call-done = f32[2,64,256]{2,1,0:T(8,128)} async-done(((f32[32,64,256]{2,1,0:T(8,128)}), f32[2,64,256]{2,1,0:T(8,128)}) %reduce-scatter.4.cloned.1.call-update) | async-done | bytes 131088 | tf_op jit(solution)/shard_map/reduce_scatter | solution.py:69
  166.5 1.9 fusion.20
  168.4 0.2 reduce-scatter.6.cloned.1.call-start
  168.7 55.2 %all-gather.2.cloned.1.call-done = bf16[32,64,256]{2,1,0:T(8,128)(2,1)} async-done(((bf16[2,64,256]{2,1,0:T(8,128)(2,1)}), bf16[32,64,256]{2,1,0:T(8,128)(2,1)}) %all-gather.2.cloned.1.call-update) | async-done | bytes 1048592 | tf_op jit(solution)/shard_map/all_gather | solution.py:76
  223.8 2.5 convolution_convert_fusion
  226.4 2.0 copy-done.1
  228.3 6.0 convert_bitcast_fusion
  234.4 1.2 copy-done.2
  235.6 5.7 fusion.12
  241.3 4.0 all-to-all-start.2
  245.3 0.3 all-reduce.4.cloned.1.call-start
  245.6 11.3 %copy.42 = bf16[256,50,256]{0,1,2:T(8,128)(2,1)} copy(bf16[256,50,256]{2,0,1:T(8,128)(2,1)} %param.17) | data formatting | bytes 13107200 | tf_op args[8]
  256.9 8.0 %copy.41 = bf16[32,256,256]{1,0,2:T(8,128)(2,1)} copy(bf16[32,256,256]{2,1,0:T(8,128)(2,1)} %copy-done.1) | data formatting | bytes 8388608 | tf_op jit(solution)/shard_map/convert_element_type | solution.py:79
  264.9 6.5 %fusion.30 = (f32[50]{0:T(128)S(1)}, bf16[32,50]{1,0:T(8,128)(2,1)S(1)}) fusion(f32[32,50]{1,0:T(8,128)S(1)} %convolution_add_fusion.1, bf16[32,256,256]{1,0,2:T(8,128)(2,1)} %copy.41, bf16[256,50,256]{0,1,2:T(8,128)(2,1)} %copy.42), kind=kOutput, calls=%fused_computation.40 | convolution fusion | flops 209731152 | bytes 10757704 | tf_op jit(solution)/shard_map/kdc,dhc->kh/dot_general | solution.py:92
  271.4 1.0 fusion.21
  272.4 0.6 copy.40
  273.1 1.7 copy.46
  274.7 0.8 convert_reduce_fusion
  275.6 1.8 convolution_bitcast_fusion
  277.4 0.0 reduce-scatter.8.cloned.1.call-start
  277.5 27.3 %reduce-scatter.6.cloned.1.call-done = bf16[64,50,256]{2,1,0:T(8,128)(2,1)} async-done(((bf16[256,50,256]{2,1,0:T(8,128)(2,1)}), bf16[64,50,256]{2,1,0:T(8,128)(2,1)}) %reduce-scatter.6.cloned.1.call-update) | async-done | bytes 1638416 | tf_op jit(solution)/shard_map/reduce_scatter | solution.py:31
  304.8 0.2 fusion.31
  305.0 76.7 %all-reduce = (f32[4096]{0:T(1024)}, f32[128,50]{0,1:T(8,128)}, f32[50]{0:T(128)}) all-reduce(f32[4096]{0:T(1024)S(1)} %get-tuple-element.29, f32[128,50]{0,1:T(8,128)S(1)} %fusion.31, f32[50]{0:T(128)S(1)} %get-tuple-element.33), channel_id=1, replica_groups=mesh['dp_0'=4,'dp_1'=4,'hyper'=16] {'dp_0','dp_1','hyper'}, use_global_device_ids=true, to_apply=%region_5.6 | all-reduce | flops 10546 | bytes 84368 | tf_op jit(solution)/shard_map/psum | solution.py:98
  381.7 191.7 %all-reduce.4.cloned.1.call-done = (f32[128,4096]{0,1:T(8,128)}, f32[512,128]{1,0:T(8,128)}) async-done(((f32[128,4096]{0,1:T(8,128)}, f32[512,128]{1,0:T(8,128)}), (f32[128,4096]{0,1:T(8,128)}, f32[512,128]{1,0:T(8,128)})) %all-reduce.4.cloned.1.call-update) | async-done | bytes 2359312 | tf_op jit(solution)/shard_map/psum | solution.py:98
  573.3 2.9 copy.44
  576.3 44.3 %reduce-scatter.8.cloned.1.call-done = bf16[16,50,256]{2,1,0:T(8,128)(2,1)} async-done(((bf16[64,50,256]{2,1,0:T(8,128)(2,1)}), bf16[16,50,256]{2,1,0:T(8,128)(2,1)}) %reduce-scatter.8.cloned.1.call-update) | async-done | bytes 409616 | tf_op jit(solution)/shard_map/reduce_scatter | solution.py:31
  620.6 2.0 copy.45
  622.6 0.7 copy.61
  (24 shorter events, 0.1 us)
Async XLA Ops:
  7.2 14.7 %copy-start = (bf16[128,4096]{1,0:T(8,128)(2,1)S(1)}, bf16[128,4096]{1,0:T(8,128)(2,1)}, u32[]{:S(2)}) copy-start(bf16[128,4096]{1,0:T(8,128)(2,1)} %param.12) | copy-start | bytes 3145732
  8.5 23.7 %all-to-all-start.1 = ((s32[16,1,2]{2,1,0:T(1,128)}), s32[16,1,2]{2,1,0:T(1,128)S(1)}, u32[]{:S(2)}, u32[]{:S(2)}) async-start(s32[16,1,2]{2,1,0:T(1,128)} %broadcast_in_dim.2), calls=%async_computation.1 | async-start | bytes 16384 | tf_op jit(solution)/shard_map/all_to_all | solution.py:14
  30.0 13.2 %copy-start.8 = (bf16[512,128]{1,0:T(8,128)(2,1)S(1)}, bf16[512,128]{1,0:T(8,128)(2,1)}, u32[]{:S(2)}) copy-start(bf16[512,128]{1,0:T(8,128)(2,1)} %param.14) | copy-start | bytes 393220
  30.0 13.4 %copy-start.5 = (bf16[128,50]{0,1:T(8,128)(2,1)S(1)}, bf16[128,50]{0,1:T(8,128)(2,1)}, u32[]{:S(2)}) copy-start(bf16[128,50]{0,1:T(8,128)(2,1)} %param.15) | copy-start | bytes 38404
  30.0 13.4 %copy-start.7 = (f32[50]{0:T(128)S(1)}, f32[50]{0:T(128)}, u32[]{:S(2)}) copy-start(f32[50]{0:T(128)} %param.16) | copy-start | bytes 604
  32.3 31.4 %all-to-all-start = ((bf16[16,2,16384]{2,1,0:T(2,128)(2,1)}), bf16[16,2,16384]{2,1,0:T(2,128)(2,1)S(1)}, u32[]{:S(2)}, u32[]{:S(2)}) async-start(bf16[16,2,16384]{2,1,0:T(2,128)(2,1)} %reshape.50), calls=%async_computation | async-start | bytes 2097152 | tf_op jit(solution)/shard_map/all_to_all | solution.py:68
  41.9 124.6 %reduce-scatter.4.cloned.1.call-start = ((), (), s32[]{:S(2)}) async-start(), calls=%async_computation.6 | async-start | bytes 2228224 | tf_op jit(solution)/shard_map/reduce_scatter | solution.py:69
  76.5 90.0 %copy-start.9 = (s32[2,64]{1,0:T(2,128)S(1)}, s32[2,64]{1,0:T(2,128)}, u32[]{:S(2)}) copy-start(s32[2,64]{1,0:T(2,128)} %param.10) | copy-start | bytes 1540
  76.6 147.3 %all-gather.2.cloned.1.call-start = ((), (), s32[]{:S(2)}) async-start(), calls=%async_computation.7 | async-start | bytes 1114112 | tf_op jit(solution)/shard_map/all_gather | solution.py:76
  168.4 136.4 %reduce-scatter.6.cloned.1.call-start = ((), (), s32[]{:S(2)}) async-start(), calls=%async_computation.8 | async-start | bytes 9175040 | tf_op jit(solution)/shard_map/reduce_scatter | solution.py:31
  226.4 2.0 copy-start.1
  234.4 1.2 copy-start.2
  241.3 31.1 %all-to-all-start.2 = ((bf16[32,64,256]{2,1,0:T(8,128)(2,1)}), bf16[32,64,256]{2,1,0:T(8,128)(2,1)S(1)}, u32[]{:S(2)}, u32[]{:S(2)}) async-start(bf16[32,64,256]{2,1,0:T(8,128)(2,1)} %fusion.12), calls=%async_computation.3 | async-start | bytes 2097152 | tf_op jit(solution)/shard_map/all_to_all | solution.py:83
  245.3 328.0 %all-reduce.4.cloned.1.call-start = ((), (), s32[]{:S(2)}) async-start(), calls=%async_computation.10 | async-start | bytes 4718592 | tf_op jit(solution)/shard_map/psum | solution.py:98
  273.0 1.7 copy-start.3
  274.7 0.8 copy-start.6
  277.4 343.2 %reduce-scatter.8.cloned.1.call-start = ((), (), s32[]{:S(2)}) async-start(), calls=%async_computation.9 | async-start | bytes 2293760 | tf_op jit(solution)/shard_map/reduce_scatter | solution.py:31
  573.3 49.3 %copy-start.4 = (f32[512,128]{1,0:T(8,128)S(1)}, f32[512,128]{1,0:T(8,128)}, u32[]{:S(2)}) copy-start(f32[512,128]{1,0:T(8,128)} %get-tuple-element.39) | copy-start | bytes 786436
Sparse Core Ops, SparseCore 0:
  76.7 89.7 reduce-scatter.3
  169.8 54.0 all-gather.1
  234.5 70.2 reduce-scatter.5
  310.7 262.5 all-reduce.3
  575.7 44.7 reduce-scatter.7
where the time goes:
time: 631 us; the launch traced here: 630 us
  waiting for transfers between devices  418 us (66%)
  blocking collectives  76.7 us (12%)
  local copies, waits for them, and re-layouts  46.5 us (7%)
  matrix products  43.7 us (7%)
  starting transfers between devices  26.8 us (4%)
  between operations  13.9 us (2%)
    psum x1, waiting for transfers between devices, local(): lax.psum((grad_weight, grad_bias, grad_table, grad_in, grad_hbias), DP_HY...  192 us
    reduce_scatter x1, waiting for transfers between devices, local(): lax.psum_scatter(jnp.einsum('krd,kdc->krc', feat_cols, head_part, preferr...  89.9 us
    psum x1, blocking collectives, local(): lax.psum((grad_weight, grad_bias, grad_table, grad_in, grad_hbias), DP_HY...  76.7 us
    reduce_scatter x2, waiting for transfers between devices, own_rows(): total = lax.psum_scatter(total, axis, scatter_dimension=0, tiled=True)  71.6 us
    all_gather x1, waiting for transfers between devices, local(): dlog_rows = lax.all_gather(dlogits, 'hyper', axis=0, tiled=True)  55.2 us
    unnamed x27, local copies, waits for them, and re-layouts  26.5 us
  transfers between devices with their start and end apart: 8, of which 6 were waited for; matrix products, arithmetic and copies ran while one was open for 10% of the time, Pallas kernels for 0%

commit v1 on v0

--- a/solution.py
+++ b/solution.py
@@ -73,7 +73,9 @@
         tiled=True,
     )
     dlogits = class_grads(logits, labels, row_count)
-    dlog_rows = lax.all_gather(dlogits, "hyper", axis=0, tiled=True)
+    dlog_rows = jnp.concatenate(
+        lax.all_to_all(jnp.stack([dlogits] * lax.axis_size("hyper")), "hyper", 0, 0), axis=0
+    )
     dhead_part = jnp.einsum(
         "krd,krc->kdc", feat_cols, dlog_rows, preferred_element_type=jnp.float32
     ).astype(jnp.bfloat16)

time: 631 us -> 607 us (0.962)
  waiting for transfers between devices: 418 us -> 375 us
  blocking collectives: 76.7 us -> 103 us
    all_gather x1 -> x0, waiting for transfers between devices: 55.2 us -> none  [local(): dlog_rows = lax.all_gather(dlogits, 'hyper', axis=0, tiled=True)]
    all_to_all x0 -> x1, blocking collectives: none -> 25.9 us  [local(): lax.all_to_all(jnp.stack([dlogits] * lax.axis_size('hyper')), 'hyper', 0, 0)]
    reduce_scatter x2, waiting for transfers between devices: 71.6 us -> 83.5 us  [own_rows(): total = lax.psum_scatter(total, axis, scatter_dimension=0, tiled=True)]
  transfers between devices with their start and end apart: 8 -> 7, of which waited for: 6 -> 5; matrix products, arithmetic and copies ran while one was open for 10% -> 11% of each run, Pallas kernels for 0% -> 0%
where the time goes in v1:
time: 607 us; the launch traced here: 606 us
  waiting for transfers between devices  375 us (62%)
  blocking collectives  103 us (17%)
  matrix products  42.5 us (7%)
  local copies, waits for them, and re-layouts  41.4 us (7%)
  starting transfers between devices  27.2 us (4%)
  between operations  13.9 us (2%)
    psum x1, waiting for transfers between devices, local(): lax.psum((grad_weight, grad_bias, grad_table, grad_in, grad_hbias), DP_HY...  192 us
    reduce_scatter x1, waiting for transfers between devices, local(): lax.psum_scatter(jnp.einsum('krd,kdc->krc', feat_cols, head_part, preferr...  89.9 us
    reduce_scatter x2, waiting for transfers between devices, own_rows(): total = lax.psum_scatter(total, axis, scatter_dimension=0, tiled=True)  83.5 us
    psum x1, blocking collectives, local(): lax.psum((grad_weight, grad_bias, grad_table, grad_in, grad_hbias), DP_HY...  76.7 us
    all_to_all x1, blocking collectives, local(): lax.all_to_all(jnp.stack([dlogits] * lax.axis_size('hyper')), 'hyper', 0, 0)  25.9 us
    unnamed x27, local copies, waits for them, and re-layouts  24.5 us
    all_to_all x1, starting transfers between devices, sent_to_all(): return lax.all_to_all(copies, axis, split_axis=0, concat_axis=0, tiled=True)  12.6 us
  transfers between devices with their start and end apart: 7, of which 5 were waited for; matrix products, arithmetic and copies ran while one was open for 11% of the time, Pallas kernels for 0%

profile of v1, /device:TPU:1, one launch (start us, length us, event | category | flops | bytes accessed | tf_op | source)
XLA Modules:
  0.0 606.0 jit_solution(4629020946109746182)
XLA Ops:
  7.2 1.3 broadcast_in_dim.2
  8.5 12.6 %all-to-all-start.1 = ((s32[16,1,2]{2,1,0:T(1,128)}), s32[16,1,2]{2,1,0:T(1,128)S(1)}, u32[]{:S(2)}, u32[]{:S(2)}) async-start(s32[16,1,2]{2,1,0:T(1,128)} %broadcast_in_dim.2), calls=%async_computation.1 | async-start | bytes 16384 | tf_op jit(solution)/shard_map/all_to_all | solution.py:14
  21.1 0.7 convert_element_type.58
  21.8 3.1 multiply_convert_fusion.1
  24.9 5.0 copy.35
  30.0 2.2 reshape.56
  32.3 9.6 %all-to-all-start = ((bf16[16,2,16384]{2,1,0:T(2,128)(2,1)}), bf16[16,2,16384]{2,1,0:T(2,128)(2,1)S(1)}, u32[]{:S(2)}, u32[]{:S(2)}) async-start(bf16[16,2,16384]{2,1,0:T(2,128)(2,1)} %reshape.56), calls=%async_computation | async-start | bytes 2097152 | tf_op jit(solution)/shard_map/all_to_all | solution.py:68
  41.9 0.0 reduce-scatter.4.cloned.1.call-start
  41.9 0.5 broadcast.20
  42.5 0.7 reduce.3
  43.1 0.1 eq.28
  43.2 0.2 convolution_convert_fusion.1
  43.4 0.1 convolution_add_fusion.1
  43.6 10.5 %fusion.9 = bf16[32,256,256]{2,0,1:T(8,128)(2,1)} fusion(bf16[256,50,256]{2,0,1:T(8,128)(2,1)} %param.17, f32[32,50]{1,0:T(8,128)S(1)} %convolution_add_fusion.1), kind=kOutput, calls=%fused_computation.12 | convolution fusion | flops 211820352 | bytes 10754304 | tf_op jit(solution)/shard_map/kh,dhc->kdc/dot_general | solution.py:65
  54.1 9.7 %all-to-all-done = bf16[16,2,16384]{2,1,0:T(2,128)(2,1)S(1)} async-done(((bf16[16,2,16384]{2,1,0:T(2,128)(2,1)}), bf16[16,2,16384]{2,1,0:T(2,128)(2,1)S(1)}, u32[]{:S(2)}, u32[]{:S(2)}) %all-to-all-start) | async-done | bytes 1048608 | tf_op jit(solution)/shard_map/all_to_all | solution.py:68
  63.7 1.3 reshape.57
  65.1 1.2 copy.36
  66.3 5.9 fusion.7
  72.2 0.0 reduce-scatter.4.cloned.1.call-update
  72.3 0.0 reduce-scatter.6.cloned.1.call-start
  72.3 89.9 %reduce-scatter.4.cloned.1.call-done = f32[2,64,256]{2,1,0:T(8,128)} async-done(((f32[32,64,256]{2,1,0:T(8,128)}), f32[2,64,256]{2,1,0:T(8,128)}) %reduce-scatter.4.cloned.1.call-update) | async-done | bytes 131088 | tf_op jit(solution)/shard_map/reduce_scatter | solution.py:69
  162.2 1.2 fusion.20
  163.4 0.1 stack.2
  163.5 25.9 %all_to_all.38 = bf16[16,2,64,256]{3,2,1,0:T(8,128)(2,1)S(1)} all-to-all(bf16[16,2,64,256]{3,2,1,0:T(8,128)(2,1)S(1)} %stack.2), channel_id=1, replica_groups=mesh['dp_0'=4,'dp_1'=4,'hyper'=16] {'hyper'}, dimensions={0} | all-to-all | bytes 2097152 | tf_op jit(solution)/shard_map/all_to_all | solution.py:77
  189.5 1.3 convolution_convert_fusion
  190.8 1.9 copy-done.2
  192.7 6.0 convert_bitcast_fusion
  198.8 5.7 fusion.12
  204.5 4.6 all-to-all-start.3
  209.1 0.3 all-reduce.4.cloned.1.call-start
  209.4 11.6 %copy.42 = bf16[256,50,256]{0,1,2:T(8,128)(2,1)} copy(bf16[256,50,256]{2,0,1:T(8,128)(2,1)} %param.17) | data formatting | bytes 13107200 | tf_op args[8]
  221.0 7.9 %copy.41 = bf16[32,256,256]{1,0,2:T(8,128)(2,1)} copy(bf16[32,256,256]{2,1,0:T(8,128)(2,1)} %copy-done.2) | data formatting | bytes 8388608 | tf_op jit(solution)/shard_map/convert_element_type | solution.py:81
  228.9 6.5 %fusion.30 = (f32[50]{0:T(128)S(1)}, bf16[32,50]{1,0:T(8,128)(2,1)S(1)}) fusion(f32[32,50]{1,0:T(8,128)S(1)} %convolution_add_fusion.1, bf16[32,256,256]{1,0,2:T(8,128)(2,1)} %copy.41, bf16[256,50,256]{0,1,2:T(8,128)(2,1)} %copy.42), kind=kOutput, calls=%fused_computation.40 | convolution fusion | flops 209731152 | bytes 10757704 | tf_op jit(solution)/shard_map/kdc,dhc->kh/dot_general | solution.py:94
  235.5 1.0 fusion.21
  236.5 0.6 copy.40
  237.1 1.7 copy.46
  238.8 0.8 convert_reduce_fusion
  239.7 1.8 convolution_bitcast_fusion
  241.5 0.0 all-reduce.4.cloned.1.call-update
  241.5 0.0 reduce-scatter.8.cloned.1.call-start
  241.5 39.3 %reduce-scatter.6.cloned.1.call-done = bf16[64,50,256]{2,1,0:T(8,128)(2,1)} async-done(((bf16[256,50,256]{2,1,0:T(8,128)(2,1)}), bf16[64,50,256]{2,1,0:T(8,128)(2,1)}) %reduce-scatter.6.cloned.1.call-update) | async-done | bytes 1638416 | tf_op jit(solution)/shard_map/reduce_scatter | solution.py:31
  280.8 0.2 fusion.31
  281.0 76.7 %all-reduce = (f32[4096]{0:T(1024)}, f32[128,50]{0,1:T(8,128)}, f32[50]{0:T(128)}) all-reduce(f32[4096]{0:T(1024)S(1)} %get-tuple-element.29, f32[128,50]{0,1:T(8,128)S(1)} %fusion.31, f32[50]{0:T(128)S(1)} %get-tuple-element.33), channel_id=1, replica_groups=mesh['dp_0'=4,'dp_1'=4,'hyper'=16] {'dp_0','dp_1','hyper'}, use_global_device_ids=true, to_apply=%region_5.6 | all-reduce | flops 10546 | bytes 84368 | tf_op jit(solution)/shard_map/psum | solution.py:100
  357.7 191.8 %all-reduce.4.cloned.1.call-done = (f32[128,4096]{0,1:T(8,128)}, f32[512,128]{1,0:T(8,128)}) async-done(((f32[128,4096]{0,1:T(8,128)}, f32[512,128]{1,0:T(8,128)}), (f32[128,4096]{0,1:T(8,128)}, f32[512,128]{1,0:T(8,128)})) %all-reduce.4.cloned.1.call-update) | async-done | bytes 2359312 | tf_op jit(solution)/shard_map/psum | solution.py:100
  549.5 3.0 copy.44
  552.5 44.3 %reduce-scatter.8.cloned.1.call-done = bf16[16,50,256]{2,1,0:T(8,128)(2,1)} async-done(((bf16[64,50,256]{2,1,0:T(8,128)(2,1)}), bf16[16,50,256]{2,1,0:T(8,128)(2,1)}) %reduce-scatter.8.cloned.1.call-update) | async-done | bytes 409616 | tf_op jit(solution)/shard_map/reduce_scatter | solution.py:31
  596.7 2.0 copy.45
  598.7 0.7 copy.61
  (23 shorter events, 0.1 us)
Async XLA Ops:
  7.2 14.7 %copy-start = (bf16[128,4096]{1,0:T(8,128)(2,1)S(1)}, bf16[128,4096]{1,0:T(8,128)(2,1)}, u32[]{:S(2)}) copy-start(bf16[128,4096]{1,0:T(8,128)(2,1)} %param.12) | copy-start | bytes 3145732
  8.5 23.7 %all-to-all-start.1 = ((s32[16,1,2]{2,1,0:T(1,128)}), s32[16,1,2]{2,1,0:T(1,128)S(1)}, u32[]{:S(2)}, u32[]{:S(2)}) async-start(s32[16,1,2]{2,1,0:T(1,128)} %broadcast_in_dim.2), calls=%async_computation.1 | async-start | bytes 16384 | tf_op jit(solution)/shard_map/all_to_all | solution.py:14
  30.0 13.2 %copy-start.8 = (bf16[512,128]{1,0:T(8,128)(2,1)S(1)}, bf16[512,128]{1,0:T(8,128)(2,1)}, u32[]{:S(2)}) copy-start(bf16[512,128]{1,0:T(8,128)(2,1)} %param.14) | copy-start | bytes 393220
  30.0 13.4 %copy-start.5 = (bf16[128,50]{0,1:T(8,128)(2,1)S(1)}, bf16[128,50]{0,1:T(8,128)(2,1)}, u32[]{:S(2)}) copy-start(bf16[128,50]{0,1:T(8,128)(2,1)} %param.15) | copy-start | bytes 38404
  30.0 13.4 %copy-start.7 = (f32[50]{0:T(128)S(1)}, f32[50]{0:T(128)}, u32[]{:S(2)}) copy-start(f32[50]{0:T(128)} %param.16) | copy-start | bytes 604
  32.3 31.5 %all-to-all-start = ((bf16[16,2,16384]{2,1,0:T(2,128)(2,1)}), bf16[16,2,16384]{2,1,0:T(2,128)(2,1)S(1)}, u32[]{:S(2)}, u32[]{:S(2)}) async-start(bf16[16,2,16384]{2,1,0:T(2,128)(2,1)} %reshape.56), calls=%async_computation | async-start | bytes 2097152 | tf_op jit(solution)/shard_map/all_to_all | solution.py:68
  41.9 120.3 %reduce-scatter.4.cloned.1.call-start = ((), (), s32[]{:S(2)}) async-start(), calls=%async_computation.7 | async-start | bytes 2228224 | tf_op jit(solution)/shard_map/reduce_scatter | solution.py:69
  72.2 89.9 %copy-start.9 = (s32[2,64]{1,0:T(2,128)S(1)}, s32[2,64]{1,0:T(2,128)}, u32[]{:S(2)}) copy-start(s32[2,64]{1,0:T(2,128)} %param.10) | copy-start | bytes 1540
  72.3 208.5 %reduce-scatter.6.cloned.1.call-start = ((), (), s32[]{:S(2)}) async-start(), calls=%async_computation.8 | async-start | bytes 9175040 | tf_op jit(solution)/shard_map/reduce_scatter | solution.py:31
  190.8 2.0 copy-start.2
  204.5 32.0 %all-to-all-start.3 = ((bf16[32,64,256]{2,1,0:T(8,128)(2,1)}), bf16[32,64,256]{2,1,0:T(8,128)(2,1)S(1)}, u32[]{:S(2)}, u32[]{:S(2)}) async-start(bf16[32,64,256]{2,1,0:T(8,128)(2,1)} %fusion.12), calls=%async_computation.4 | async-start | bytes 2097152 | tf_op jit(solution)/shard_map/all_to_all | solution.py:85
  209.1 340.4 %all-reduce.4.cloned.1.call-start = ((), (), s32[]{:S(2)}) async-start(), calls=%async_computation.10 | async-start | bytes 4718592 | tf_op jit(solution)/shard_map/psum | solution.py:100
  237.1 1.7 copy-start.3
  238.8 0.8 copy-start.6
  241.5 355.2 %reduce-scatter.8.cloned.1.call-start = ((), (), s32[]{:S(2)}) async-start(), calls=%async_computation.9 | async-start | bytes 2293760 | tf_op jit(solution)/shard_map/reduce_scatter | solution.py:31
  549.5 50.0 %copy-start.1 = (bf16[128,4096]{1,0:T(8,128)(2,1)S(1)}, bf16[128,4096]{1,0:T(8,128)(2,1)}, u32[]{:S(2)}) copy-start(bf16[128,4096]{1,0:T(8,128)(2,1)} %param.12) | copy-start | bytes 3145732
  549.5 49.3 %copy-start.4 = (f32[512,128]{1,0:T(8,128)S(1)}, f32[512,128]{1,0:T(8,128)}, u32[]{:S(2)}) copy-start(f32[512,128]{1,0:T(8,128)} %get-tuple-element.39) | copy-start | bytes 786436
Sparse Core Ops, SparseCore 0:
  72.4 89.7 reduce-scatter.3
  198.9 81.8 reduce-scatter.5
  286.9 262.5 all-reduce.3
  551.9 44.7 reduce-scatter.7
